TPU v7x, 8 devices: a whole 2x2x1 slice. The times are simulated.
8 devices in a mesh: fsdp: 8 (over z, y, x, core).
Axes of the slice: x: 2, y: 2, z: 1, core: 2. Of those that a mesh axis runs over, the one named last changes fastest.
Arguments:
- token_ids: int32 [64, 1024], P('fsdp')
- embed_table: bfloat16 [32000, 2048], P('fsdp')
- norm_gain: bfloat16 [2048], P('fsdp')
- w_query: bfloat16 [2048, 32, 64], P('fsdp')
- w_key: bfloat16 [2048, 4, 64], P('fsdp')
- w_value: bfloat16 [2048, 4, 64], P('fsdp')
- w_out: bfloat16 [2048, 2048], P('fsdp')
- grad_out: bfloat16 [64, 1024, 2048], P('fsdp')
Outputs:
- output 1: bfloat16 [64, 1024, 2048], P('fsdp')
- output 2: float32 [32000, 2048], P('fsdp')
- output 3: float32 [2048], P('fsdp')
- output 4: float32 [2048, 32, 64], P('fsdp')
- output 5: float32 [2048, 4, 64], P('fsdp')
- output 6: float32 [2048, 4, 64], P('fsdp')
- output 7: float32 [2048, 2048], P('fsdp')
All inputs are finite; a program needn't handle non-finite values.
Results may differ from a plain program's by a relative error of at most 0.00862023.
Values are sent between devices in bfloat16 or wider.
A program may use at most 1 GiB of HBM per device.

v0:
```python
import functools

import jax
import jax.numpy as jnp
from jax import lax
from jax.experimental import pallas as pl
from jax.experimental.pallas import tpu as pltpu
from jax.sharding import PartitionSpec as P


ROPE_THETA = 500000.0
NORM_EPS = 1e-5
WINDOWS = 4
LANES = 128
ROWS = 256
PARTS = 4
RUN = 128

NT = (((1,), (1,)), ((), ()))
F32 = jnp.float32
BF16 = jnp.bfloat16


def split_kernel(table_ref, out_ref, wide):
    rows, width = table_ref.shape
    slabs = width // LANES
    for j in range(slabs):
        wide[pl.ds(j, rows, stride=slabs), :] = table_ref[:, j * LANES : (j + 1) * LANES].astype(F32)
    out_ref[...] = wide[...].reshape(rows, slabs, LANES).astype(BF16)


def split_rows(table, block=200):
    rows, width = table.shape
    slabs = width // LANES
    return pl.pallas_call(
        split_kernel,
        grid=(rows // block,),
        out_shape=jax.ShapeDtypeStruct((rows, slabs, LANES), BF16),
        in_specs=[pl.BlockSpec((block, width), lambda i: (i, 0))],
        out_specs=pl.BlockSpec((block, slabs, LANES), lambda i: (i, 0, 0)),
        scratch_shapes=[pltpu.VMEM((block * slabs, LANES), F32)],
        cost_estimate=pl.CostEstimate(flops=rows * width, bytes_accessed=4 * rows * width, transcendentals=0),
        name='split_rows',
    )(table)


def join_kernel(scale, part_ref, *refs):
    out_ref, wide = refs[-2:]
    rows, width = out_ref.shape
    slabs = width // LANES
    wide[...] = part_ref[...].astype(F32).reshape(rows * slabs, LANES) * scale
    for j in range(slabs):
        out_ref[:, j * LANES : (j + 1) * LANES] = wide[pl.ds(j, rows, stride=slabs), :]


def join_rows(part, whole, index, count, scale, block=200):
    rows, slabs, _ = part.shape
    width = slabs * LANES
    steps = rows // block
    in_specs = [pl.BlockSpec((block, slabs, LANES), lambda i: (i, 0, 0))]
    operands = [part]
    aliases = {}
    if whole is not None:
        in_specs.append(pl.BlockSpec(memory_space=pl.ANY))
        operands.append(whole)
        aliases = {1: 0}
    return pl.pallas_call(
        functools.partial(join_kernel, scale),
        grid=(steps,),
        out_shape=jax.ShapeDtypeStruct((rows * count, width), F32),
        in_specs=in_specs,
        out_specs=pl.BlockSpec((block, width), lambda i: (index * steps + i, 0)),
        scratch_shapes=[pltpu.VMEM((block * slabs, LANES), F32)],
        input_output_aliases=aliases,
        cost_estimate=pl.CostEstimate(flops=rows * width, bytes_accessed=6 * rows * width, transcendentals=0),
        name='join_rows',
    )(*operands)


def embed_kernel(ids_ref, table_ref, gain_ref, weight_ref, x_ref, normed_ref, raw_ref, fetched, wide, sems):
    step, steps = pl.program_id(0), pl.num_programs(0)
    rows, width = x_ref.shape
    slabs = width // LANES

    def fetch(block, slot):
        def one(t, carry):
            pltpu.make_async_copy(table_ref.at[ids_ref[block * rows + t]], fetched.at[slot, t], sems.at[slot]).start()
            return carry

        lax.fori_loop(0, rows, one, 0, unroll=8)

    @pl.when(step == 0)
    def _():
        fetch(0, 0)

    @pl.when(step + 1 < steps)
    def _():
        fetch(step + 1, lax.rem(step + 1, 2))

    slot = lax.rem(step, 2)
    pltpu.make_async_copy(table_ref.at[pl.ds(0, rows)], fetched.at[slot], sems.at[slot]).wait()
    wide[...] = fetched[slot].astype(F32).reshape(rows * slabs, LANES)
    square = jnp.zeros((rows, LANES), F32)
    for j in range(slabs):
        x_part = wide[pl.ds(j, rows, stride=slabs), :]
        square += x_part * x_part
        x_ref[:, j * LANES : (j + 1) * LANES] = x_part.astype(BF16)
    scale = lax.rsqrt(jnp.sum(square, axis=1, keepdims=True) * (1.0 / width) + NORM_EPS)
    for j in range(slabs):
        cols = slice(j * LANES, (j + 1) * LANES)
        normed_ref[:, cols] = (x_ref[:, cols].astype(F32) * scale * gain_ref[:, cols]).astype(BF16)
    raw_ref[0] = lax.dot_general(weight_ref[...], normed_ref[...], NT, preferred_element_type=F32)


def embed_project(ids, table, gain, weight_t):
    tokens = ids.shape[0]
    slabs = table.shape[1]
    features, width = weight_t.shape
    steps = tokens // ROWS
    return pl.pallas_call(
        embed_kernel,
        grid_spec=pltpu.PrefetchScalarGridSpec(
            num_scalar_prefetch=1,
            grid=(steps,),
            in_specs=[
                pl.BlockSpec(memory_space=pl.ANY),
                pl.BlockSpec((1, width), lambda i, ids: (0, 0)),
                pl.BlockSpec((features, width), lambda i, ids: (0, 0)),
            ],
            out_specs=[
                pl.BlockSpec((ROWS, width), lambda i, ids: (i, 0)),
                pl.BlockSpec((ROWS, width), lambda i, ids: (i, 0)),
                pl.BlockSpec((1, features, ROWS), lambda i, ids: (i, 0, 0)),
            ],
            scratch_shapes=[
                pltpu.VMEM((2, ROWS, slabs, LANES), BF16),
                pltpu.VMEM((ROWS * slabs, LANES), F32),
                pltpu.SemaphoreType.DMA((2,)),
            ],
        ),
        out_shape=[
            jax.ShapeDtypeStruct((tokens, width), BF16),
            jax.ShapeDtypeStruct((tokens, width), BF16),
            jax.ShapeDtypeStruct((steps, features, ROWS), F32),
        ],
        cost_estimate=pl.CostEstimate(flops=2 * tokens * width * features, bytes_accessed=tokens * (6 * width + 4 * features), transcendentals=tokens),
        name='embed_project',
    )(ids, table, gain, weight_t)


def rotate(values, cosine, sine):
    half = values.shape[0] // 2
    first, second = values[:half], values[half:]
    return jnp.concatenate([first * cosine - second * sine, second * cosine + first * sine], axis=0)


def rotate_back(values, cosine, sine):
    half = values.shape[0] // 2
    first, second = values[:half], values[half:]
    return jnp.concatenate([first * cosine + second * sine, second * cosine - first * sine], axis=0)


def head_norm(values):
    scale = lax.rsqrt(jnp.mean(values * values, axis=0, keepdims=True) + NORM_EPS)
    return values * scale, scale


def head_norm_back(grads, unit, scale):
    return scale * (grads - unit * jnp.mean(unit * grads, axis=0, keepdims=True))


def attention_kernel(group, dim, raw_ref, dmix_ref, cos_ref, sin_ref, mix_ref, draw_ref):
    tokens = raw_ref.shape[2]
    half = tokens // 2
    cosine, sine = cos_ref[...], sin_ref[...]
    k_unit, k_scale = head_norm(rotate(raw_ref[0, group * dim : (group + 1) * dim, :], cosine, sine))
    key_t = k_unit.astype(BF16)
    key_f = key_t.astype(F32) * dim**-0.5
    key_small_t = key_f.astype(BF16)
    key_small = key_f.T.astype(BF16)
    value_f = raw_ref[0, (group + 1) * dim : (group + 2) * dim, :].astype(BF16)
    value_t = value_f
    value = value_f.astype(F32).T.astype(BF16)
    keys_at = lax.broadcasted_iota(jnp.int32, (half, half), 0)
    queries_at = lax.broadcasted_iota(jnp.int32, (half, half), 1)
    causal = queries_at >= keys_at
    empty = jnp.zeros((half, half), BF16)
    d_key = jnp.zeros((dim, tokens), F32)
    d_value = jnp.zeros((dim, tokens), F32)
    for head in range(group):
        rows = slice(head * dim, (head + 1) * dim)
        q_unit, q_scale = head_norm(rotate(raw_ref[0, rows, :], cosine, sine))
        query_t = q_unit.astype(BF16)
        d_out = dmix_ref[rows, :]
        scores = jnp.dot(key_small, query_t, preferred_element_type=F32)
        d_probs = jnp.dot(value, d_out, preferred_element_type=F32)
        early = jnp.where(causal, jnp.exp(scores[:half, :half]), 0.0)
        cross = jnp.exp(scores[:half, half:])
        late = jnp.where(causal, jnp.exp(scores[half:, half:]), 0.0)
        early_inv = 1.0 / jnp.sum(early, axis=0, keepdims=True)
        late_inv = 1.0 / (jnp.sum(cross, axis=0, keepdims=True) + jnp.sum(late, axis=0, keepdims=True))
        early, cross, late = early * early_inv, cross * late_inv, late * late_inv
        probs = jnp.concatenate(
            [
                jnp.concatenate([early.astype(BF16), cross.astype(BF16)], axis=1),
                jnp.concatenate([empty, late.astype(BF16)], axis=1),
            ],
            axis=0,
        )
        mix_ref[rows, :] = jnp.dot(value_t, probs, preferred_element_type=F32).astype(BF16)
        d_early, d_cross, d_late = d_probs[:half, :half], d_probs[:half, half:], d_probs[half:, half:]
        early_dot = jnp.sum(early * d_early, axis=0, keepdims=True)
        late_dot = jnp.sum(cross * d_cross, axis=0, keepdims=True) + jnp.sum(late * d_late, axis=0, keepdims=True)
        d_scores = jnp.concatenate(
            [
                jnp.concatenate([(early * (d_early - early_dot)).astype(BF16), (cross * (d_cross - late_dot)).astype(BF16)], axis=1),
                jnp.concatenate([empty, (late * (d_late - late_dot)).astype(BF16)], axis=1),
            ],
            axis=0,
        )
        d_query = jnp.dot(key_small_t, d_scores, preferred_element_type=F32)
        d_key += lax.dot_general(query_t, d_scores, NT, preferred_element_type=F32)
        d_value += lax.dot_general(d_out, probs, NT, preferred_element_type=F32)
        draw_ref[rows, :] = rotate_back(head_norm_back(d_query, q_unit, q_scale), cosine, sine).astype(BF16)
    d_key = rotate_back(head_norm_back(d_key * dim**-0.5, k_unit, k_scale), cosine, sine)
    draw_ref[group * dim : (group + 1) * dim, :] = d_key.astype(BF16)
    draw_ref[(group + 1) * dim :, :] = d_value.astype(BF16)


def attention(raw, d_mixed_t, cosine, sine, kv_heads, group, dim):
    steps, features, tokens = raw.shape
    block = features // kv_heads
    width = group * dim
    pairs = steps * kv_heads * group * tokens * tokens
    return pl.pallas_call(
        functools.partial(attention_kernel, group, dim),
        grid=(steps, kv_heads),
        in_specs=[
            pl.BlockSpec((1, block, tokens), lambda w, k: (w, k, 0)),
            pl.BlockSpec((width, tokens), lambda w, k: (k, w)),
            pl.BlockSpec((dim // 2, tokens), lambda w, k: (0, w % WINDOWS)),
            pl.BlockSpec((dim // 2, tokens), lambda w, k: (0, w % WINDOWS)),
        ],
        out_specs=[
            pl.BlockSpec((width, tokens), lambda w, k: (k, w)),
            pl.BlockSpec((block, tokens), lambda w, k: (k, w)),
        ],
        out_shape=[
            jax.ShapeDtypeStruct((width * kv_heads, steps * tokens), BF16),
            jax.ShapeDtypeStruct((features, steps * tokens), BF16),
        ],
        cost_estimate=pl.CostEstimate(flops=12 * pairs * dim, bytes_accessed=8 * raw.size, transcendentals=pairs),
        name='attention',
    )(raw, d_mixed_t, cosine, sine)


def input_grad_kernel(place_ref, draw_ref, weight_ref, x_ref, dh_ref, gain_ref, sorted_ref, dgain_ref, d_normed, wide, sems):
    step, steps = pl.program_id(0), pl.num_programs(0)
    rows, width = x_ref.shape
    slabs = width // LANES
    slot = lax.rem(step, 2)

    def drain(which):
        pltpu.make_async_copy(wide.at[which], sorted_ref.at[pl.ds(0, rows * slabs)], sems.at[which]).wait()

    d_normed[...] = jnp.dot(draw_ref[...].T, weight_ref[...], preferred_element_type=F32)
    square = jnp.zeros((rows, LANES), F32)
    cross = jnp.zeros((rows, LANES), F32)
    for j in range(slabs):
        cols = slice(j * LANES, (j + 1) * LANES)
        x_part = x_ref[:, cols].astype(F32)
        square += x_part * x_part
        cross += x_part * d_normed[:, cols] * gain_ref[:, cols]
    scale = lax.rsqrt(jnp.sum(square, axis=1, keepdims=True) * (1.0 / width) + NORM_EPS)
    pull = jnp.sum(cross, axis=1, keepdims=True) * (1.0 / width) * scale * scale

    @pl.when(step == 0)
    def _():
        dgain_ref[...] = jnp.zeros_like(dgain_ref)

    @pl.when(step >= 2)
    def _():
        drain(slot)

    for j in range(slabs):
        cols = slice(j * LANES, (j + 1) * LANES)
        x_part = x_ref[:, cols].astype(F32)
        d_part = d_normed[:, cols]
        dx_part = dh_ref[:, cols].astype(F32) + scale * (d_part * gain_ref[:, cols] - x_part * pull)
        wide[slot, pl.ds(j, rows, stride=slabs), :] = dx_part
        terms = d_part * (x_part * scale)
        dgain_ref[:, cols] += jnp.sum(terms.reshape(rows // 8, 8, LANES), axis=0)

    def one(t, carry):
        source = wide.at[slot, pl.ds(pl.multiple_of(t * slabs, slabs), slabs)]
        start = pl.multiple_of(place_ref[step * rows + t] * slabs, slabs)
        pltpu.make_async_copy(source, sorted_ref.at[pl.ds(start, slabs)], sems.at[slot]).start()
        return carry

    lax.fori_loop(0, rows, one, 0, unroll=8)

    @pl.when(step == steps - 1)
    def _():
        drain(1 - slot)
        drain(slot)


def input_grad(place, draw_t, weight_t, x, dh, gain, spare):
    tokens, width = x.shape
    slabs = width // LANES
    features = draw_t.shape[0]
    steps = tokens // ROWS
    return pl.pallas_call(
        input_grad_kernel,
        grid_spec=pltpu.PrefetchScalarGridSpec(
            num_scalar_prefetch=1,
            grid=(steps,),
            in_specs=[
                pl.BlockSpec((features, ROWS), lambda i, place: (0, i)),
                pl.BlockSpec((features, width), lambda i, place: (0, 0)),
                pl.BlockSpec((ROWS, width), lambda i, place: (i, 0)),
                pl.BlockSpec((ROWS, width), lambda i, place: (i, 0)),
                pl.BlockSpec((1, width), lambda i, place: (0, 0)),
            ],
            out_specs=[
                pl.BlockSpec(memory_space=pl.ANY),
                pl.BlockSpec((8, width), lambda i, place: (0, 0)),
            ],
            scratch_shapes=[
                pltpu.VMEM((ROWS, width), F32),
                pltpu.VMEM((2, ROWS * slabs, LANES), F32),
                pltpu.SemaphoreType.DMA((2,)),
            ],
        ),
        out_shape=[
            jax.ShapeDtypeStruct(((tokens + spare) * slabs, LANES), F32),
            jax.ShapeDtypeStruct((8, width), F32),
        ],
        cost_estimate=pl.CostEstimate(flops=2 * tokens * width * features, bytes_accessed=tokens * (8 * width + 2 * features), transcendentals=tokens),
        name='input_grad',
    )(place, draw_t, weight_t, x, dh, gain)


def table_grad_kernel(bounds_ref, same_ref, target_ref, sorted_ref, zero_ref, out_ref, fetched, summed, in_sems, out_sems):
    del zero_ref
    slabs = out_ref.shape[1]
    first, last = bounds_ref[0], bounds_ref[1]
    steps = lax.div(last - first + (RUN - 1), RUN)

    def fetch(step, slot):
        start = pl.multiple_of((first + step * RUN) * slabs, slabs)
        return pltpu.make_async_copy(sorted_ref.at[pl.ds(start, RUN * slabs)], fetched.at[slot], in_sems.at[slot])

    def drain(count, slot):
        for bit in range(RUN.bit_length()):

            @pl.when(lax.rem(lax.div(count, 1 << bit), 2) == 1)
            def _():
                pltpu.make_async_copy(summed.at[slot, pl.ds(0, 1 << bit)], out_ref.at[pl.ds(0, 1 << bit)], out_sems.at[slot]).wait()

    @pl.when(steps > 0)
    def _():
        fetch(0, 0).start()

    def step_body(step, carry):
        total, older, newer = carry
        slot = lax.rem(step, 2)

        @pl.when(step + 1 < steps)
        def _():
            fetch(step + 1, 1 - slot).start()

        fetch(step, slot).wait()
        drain(older, slot)
        base = first + step * RUN

        def add(t, total):
            row = fetched[slot, pl.ds(pl.multiple_of(t * slabs, slabs), slabs), :]
            total = row + jnp.where(same_ref[base + t] == 1, total, 0.0)
            summed[slot, t] = total.astype(BF16)
            return total

        total = lax.fori_loop(0, RUN, add, total, unroll=8)

        def send(t, count):
            target = target_ref[base + t]
            wanted = jnp.logical_and(target >= 0, base + t < last)

            @pl.when(wanted)
            def _():
                pltpu.make_async_copy(summed.at[slot, t], out_ref.at[target], out_sems.at[slot]).start()

            return count + wanted.astype(jnp.int32)

        count = lax.fori_loop(0, RUN, send, jnp.int32(0), unroll=8)
        return total, newer, count

    zero = jnp.int32(0)
    _, older, newer = lax.fori_loop(0, steps, step_body, (jnp.zeros((slabs, LANES), F32), zero, zero))
    drain(older, lax.rem(steps, 2))
    drain(newer, lax.rem(steps + 1, 2))


def table_grad(bounds, same, target, sorted_rows, zero_part):
    rows, slabs, _ = zero_part.shape
    return pl.pallas_call(
        table_grad_kernel,
        grid_spec=pltpu.PrefetchScalarGridSpec(
            num_scalar_prefetch=3,
            grid=(),
            in_specs=[pl.BlockSpec(memory_space=pl.ANY), pl.BlockSpec(memory_space=pl.ANY)],
            out_specs=pl.BlockSpec(memory_space=pl.ANY),
            scratch_shapes=[
                pltpu.VMEM((2, RUN * slabs, LANES), F32),
                pltpu.VMEM((2, RUN, slabs, LANES), BF16),
                pltpu.SemaphoreType.DMA((2,)),
                pltpu.SemaphoreType.DMA((2,)),
            ],
        ),
        out_shape=jax.ShapeDtypeStruct((rows, slabs, LANES), BF16),
        input_output_aliases={4: 0},
        cost_estimate=pl.CostEstimate(flops=sorted_rows.size // PARTS, bytes_accessed=6 * sorted_rows.size // PARTS, transcendentals=0),
        name='table_grad',
    )(bounds, same, target, sorted_rows, zero_part)


def zero_kernel(*refs):
    *out_refs, block, sem = refs
    block[...] = jnp.zeros_like(block)
    rows = block.shape[0]
    copies = [pltpu.make_async_copy(block, ref.at[pl.ds(start, rows)], sem) for ref in out_refs for start in range(0, ref.shape[0], rows)]
    for copy in copies:
        copy.start()
    for copy in copies:
        copy.wait()


def zero_tables(count, rows, slabs, block=400):
    return pl.pallas_call(
        zero_kernel,
        out_shape=[jax.ShapeDtypeStruct((rows, slabs, LANES), BF16)] * count,
        out_specs=[pl.BlockSpec(memory_space=pl.ANY)] * count,
        scratch_shapes=[pltpu.VMEM((block, slabs, LANES), BF16), pltpu.SemaphoreType.DMA],
        cost_estimate=pl.CostEstimate(flops=count * rows * slabs * LANES, bytes_accessed=2 * count * rows * slabs * LANES, transcendentals=0),
        name='zero_tables',
    )()


def solution(mesh):
    devices = mesh.shape['fsdp']

    def device_step(token_ids, embed_table, norm_gain, w_query, w_key, w_value, w_out, grad_out):
        batch, seq_len = token_ids.shape
        table_rows, width = embed_table.shape
        heads, dim = w_query.shape[1], w_query.shape[2]
        kv_heads = w_key.shape[1]
        group = heads // kv_heads
        tokens = batch * seq_len
        slabs = width // LANES
        ids = token_ids.reshape(tokens)
        dh = grad_out.reshape(tokens, width)

        def grouped(w, count):
            return w.transpose(1, 2, 0).reshape(kv_heads, count * dim, -1)

        weight_part = jnp.concatenate([grouped(w_query, group), grouped(w_key, 1), grouped(w_value, 1)], axis=1)
        weight_part = weight_part.reshape(-1, weight_part.shape[-1])
        wout_full = lax.all_gather(w_out, 'fsdp', axis=0, tiled=True)
        weight_t = lax.all_gather(weight_part, 'fsdp', axis=1, tiled=True)
        gain = lax.all_gather(norm_gain, 'fsdp', axis=0, tiled=True).astype(F32).reshape(1, width)
        table = lax.all_gather(split_rows(embed_table), 'fsdp', axis=0, tiled=True)

        piece = table_rows // PARTS
        part_rows = piece * devices
        local = ids % table_rows
        key = (local // piece) * part_rows + (ids // table_rows) * piece + local % piece
        count = jnp.arange(tokens, dtype=jnp.int32)
        sorted_key, order = lax.sort((key, count), num_keys=1)
        _, place = lax.sort((order, count), num_keys=1)
        outside = jnp.full((1,), -1, jnp.int32)
        same = (sorted_key == jnp.concatenate([outside, sorted_key[:-1]])).astype(jnp.int32)
        ends = sorted_key != jnp.concatenate([sorted_key[1:], outside])
        target = jnp.where(ends, sorted_key % part_rows, -1)
        spare = jnp.zeros((RUN,), jnp.int32)
        same = jnp.concatenate([same, spare])
        target = jnp.concatenate([target, spare - 1])
        bounds = jnp.sum(key[None, :] < part_rows * jnp.arange(PARTS + 1, dtype=jnp.int32)[:, None], axis=1, dtype=jnp.int32)

        half = dim // 2
        frequency = ROPE_THETA ** (-2.0 * jnp.arange(half, dtype=F32) / dim)
        angles = frequency[:, None] * jnp.arange(seq_len, dtype=F32)[None, :]
        cosine, sine = jnp.cos(angles), jnp.sin(angles)

        d_mixed_t = lax.dot_general(wout_full, dh, NT, preferred_element_type=F32).astype(BF16)
        zero_parts = zero_tables(PARTS, part_rows, slabs)
        d_mixed_t, *zero_parts = lax.optimization_barrier((d_mixed_t, *zero_parts))

        x, normed, raw = embed_project(ids, table, gain, weight_t)
        mixed_t, draw_t = attention(raw, d_mixed_t, cosine, sine, kv_heads, group, dim)
        sorted_rows, dgain = input_grad(place, draw_t, weight_t, x, dh, gain, RUN)
        parts = [table_grad(bounds[k : k + 2], same, target, sorted_rows, zero_parts[k]) for k in range(PARTS)]
        shares = []
        for k in range(PARTS):
            shares.append(lax.psum_scatter(parts[k], 'fsdp', scatter_dimension=0, tiled=True))
        grad_table = None
        for k in range(PARTS):
            grad_table = join_rows(shares[k], grad_table, k, PARTS, 1.0 / devices)

        mixed_t, draw_t, *_ = lax.optimization_barrier((mixed_t, draw_t, *parts))
        grad_weight = jnp.dot(draw_t, normed, preferred_element_type=F32).astype(BF16)
        grad_weight = lax.psum_scatter(grad_weight, 'fsdp', scatter_dimension=1, tiled=True)
        grad_weight = grad_weight.astype(F32) / devices
        grad_wout = jnp.dot(mixed_t, dh, preferred_element_type=F32).astype(BF16)
        grad_wout = lax.psum_scatter(grad_wout, 'fsdp', scatter_dimension=0, tiled=True)
        grad_wout = grad_wout.astype(F32) / devices
        hidden = x.astype(F32) + lax.dot_general(mixed_t, wout_full, (((0,), (0,)), ((), ())), preferred_element_type=F32)
        hidden = hidden.astype(BF16).reshape(batch, seq_len, width)
        grad_gain = lax.psum_scatter(jnp.sum(dgain, axis=0), 'fsdp', scatter_dimension=0, tiled=True) / devices

        grad_weight = grad_weight.reshape(kv_heads, (group + 2) * dim, -1)

        def ungrouped(part, count):
            return part.reshape(kv_heads * count, dim, -1).transpose(2, 0, 1)

        grad_query = ungrouped(grad_weight[:, : group * dim], group)
        grad_key = ungrouped(grad_weight[:, group * dim : (group + 1) * dim], 1)
        grad_value = ungrouped(grad_weight[:, (group + 1) * dim :], 1)
        return hidden, grad_table, grad_gain, grad_query, grad_key, grad_value, grad_wout

    tokens = P('fsdp', None, None)
    matrix = P('fsdp', None)
    vector = P('fsdp')
    return jax.shard_map(device_step, mesh=mesh, in_specs=(matrix, matrix, vector, tokens, tokens, tokens, matrix, tokens), out_specs=(tokens, matrix, vector, tokens, tokens, tokens, matrix), check_vma=False)
```

profile of v0, /device:TPU:0, one launch (start us, length us, event | category | flops | bytes accessed | tf_op | source)
XLA Modules:
  0.0 2562.4 jit_solution(17933106020127052598)
XLA Ops:
  7.2 0.7 all-gather.9.cloned.1.call-update
  8.0 2.5 pad_maximum_fusion
  10.6 25.9 %split_rows.1 = bf16[4000,16,128]{2,1,0:T(8,128)(2,1)} custom-call(bf16[4000,2048]{1,0:T(8,128)(2,1)} %table_ref.1), custom_call_target="tpu_custom_call" | custom-call | flops 8192000 | bytes 32768000 | tf_op jit(solution)/shard_map/split_rows/pallas_call | solution.py:35
  36.5 0.6 copy.26
  37.1 12.6 all-gather
  49.8 0.6 convert.3.gain_ref
  50.4 0.1 fusion.4
  50.5 6.2 sort.30
  56.6 0.1 fusion.9
  56.7 0.1 fusion.6
  56.8 0.6 concatenate.22.target_ref
  57.4 6.8 sort.31
  64.2 43.1 %zero_tables.1 = (bf16[8000,16,128]{2,1,0:T(8,128)(2,1)}, bf16[8000,16,128]{2,1,0:T(8,128)(2,1)}, bf16[8000,16,128]{2,1,0:T(8,128)(2,1)}, bf16[8000,16,128]{2,1,0:T(8,128)(2,1)}) custom-call(), custom_call_target="tpu_custom_call" | custom-call | flops 65536000 | bytes 131072000 | tf_op jit(solution)/shard_map/zero_tables/pallas_call | solution.py:439
  107.3 0.2 convert_reduce_fusion
  107.6 0.7 fusion.10
  108.2 0.1 add_compare_fusion
  108.3 0.6 pad_convert_fusion.same_ref
  108.9 1.2 fusion
  110.2 78.3 %convolution_convert_fusion.dmix_ref = bf16[2048,8192]{1,0:T(8,128)(2,1)} fusion(bf16[2048,2048]{1,0:T(8,128)(2,1)} %all-gather.9.cloned.1.call-done, bf16[8192,2048]{1,0:T(8,128)(2,1)} %bitcast.43), kind=kOutput, calls=%fused_computation.1 | convolution fusion | flops 68736253952 | bytes 75497472 | tf_op jit(solution)/shard_map/dot_general | solution.py:494
  188.5 505.3 %all-gather.5.cloned.1.call-done.table_ref = bf16[32000,16,128]{2,1,0:T(8,128)(2,1)} async-done(((bf16[4000,16,128]{2,1,0:T(8,128)(2,1)}), bf16[32000,16,128]{2,1,0:T(8,128)(2,1)}) %all-gather.5.cloned.1.call-update) | async-done | bytes 131072016 | tf_op jit(solution)/shard_map/all_gather | solution.py:471
  693.8 155.1 %embed_project.1 = (bf16[8192,2048]{1,0:T(8,128)(2,1)}, bf16[8192,2048]{1,0:T(8,128)(2,1)}, f32[32,2560,256]{2,1,0:T(8,128)}) custom-call(s32[8192]{0:T(1024)} %bitcast.41, bf16[32000,16,128]{2,1,0:T(8,128)(2,1)} %all-gather.5.cloned.1.call-done.table_ref, f32[1,2048]{1,0:T(1,128)} %convert.3.gain_ref, bf16[2560,2048]{1,0:T(8,128)(2,1)} %all-gather.7.cloned.1.call-done.weight_ref), custom_call_target="tpu_custom_call" | custom-call | flops 85899345920 | bytes 184549376 | tf_op jit(solution)/shard_map/embed_project/pallas_call | solution.py:120
  848.9 394.5 %attention.1 = (bf16[2048,8192]{1,0:T(8,128)(2,1)}, bf16[2560,8192]{1,0:T(8,128)(2,1)}) custom-call(f32[32,2560,256]{2,1,0:T(8,128)} %get-tuple-element.29.raw_ref, bf16[2048,8192]{1,0:T(8,128)(2,1)} %convolution_convert_fusion.dmix_ref, f32[32,1024]{1,0:T(8,128)} %get-tuple-element.58.cos_ref, f32[32,1024]{1,0:T(8,128)} %get-tuple-element.57.sin_ref), custom_call_target="tpu_custom_call" | custom-call | flops 51539607552 | bytes 167772160 | tf_op jit(solution)/shard_map/attention/pallas_call | solution.py:235
  1243.4 174.0 %input_grad.1 = (f32[133120,128]{1,0:T(8,128)}, f32[8,2048]{1,0:T(8,128)}) custom-call(s32[8192]{0:T(1024)} %get-tuple-element.39.place_ref, bf16[2560,8192]{1,0:T(8,128)(2,1)} %get-tuple-element.47.draw_ref, bf16[2560,2048]{1,0:T(8,128)(2,1)} %all-gather.7.cloned.1.call-done.weight_ref, bf16[8192,2048]{1,0:T(8,128)(2,1)} %get-tuple-element.28.x_ref, ...), custom_call_target="tpu_custom_call" | custom-call | flops 85899345920 | bytes 176160768 | tf_op jit(solution)/shard_map/input_grad/pallas_call | solution.py:313
  1417.4 22.1 table_grad.4
  1439.5 22.8 table_grad.5
  1462.4 20.9 table_grad.6
  1483.3 19.7 table_grad.7
  1503.0 79.6 %convolution_convert_fusion.2 = bf16[2048,2048]{1,0:T(8,128)(2,1)} fusion(bf16[2048,8192]{1,0:T(8,128)(2,1)} %get-tuple-element.45, bf16[8192,2048]{1,0:T(8,128)(2,1)} %bitcast.45), kind=kOutput, calls=%fused_computation.3 | convolution fusion | flops 68723671040 | bytes 75497472 | tf_op jit(solution)/shard_map/dot_general | solution.py:513
  1582.7 100.7 %convolution_convert_fusion.1 = bf16[2560,2048]{1,0:T(8,128)(2,1)} fusion(bf16[2560,8192]{1,0:T(8,128)(2,1)} %get-tuple-element.47.draw_ref, bf16[8192,2048]{1,0:T(8,128)(2,1)} %get-tuple-element.48), kind=kOutput, calls=%fused_computation.2 | convolution fusion | flops 85904588800 | bytes 85983232 | tf_op jit(solution)/shard_map/dot_general | solution.py:510
  1683.4 0.5 reduce-scatter.13.cloned.1.call-update
  1684.0 0.7 reduce-scatter.11.cloned.1.call-update
  1684.7 0.7 reduce-scatter.9.cloned.1.call-update
  1685.5 0.7 reduce-scatter.7.cloned.1.call-update
  1686.2 23.0 all-reduce.2
  1709.2 0.6 dynamic-slice_multiply_fusion
  1709.8 80.5 %add_convert_fusion = bf16[8192,2048]{1,0:T(8,128)(2,1)} fusion(bf16[8192,2048]{1,0:T(8,128)(2,1)} %get-tuple-element.28.x_ref, bf16[2048,8192]{1,0:T(8,128)(2,1)} %get-tuple-element.45, bf16[2048,2048]{1,0:T(8,128)(2,1)} %all-gather.9.cloned.1.call-done), kind=kOutput, calls=%fused_computation | convolution fusion | flops 68769808384 | bytes 109051904 | tf_op jit(solution)/shard_map/dot_general | solution.py:516
  1790.4 3.0 convert_multiply_fusion.1
  1793.4 1.7 convert_multiply_fusion
  1795.1 1.5 slice.36
  1796.6 0.8 slice_bitcast_fusion
  1797.4 158.2 %reduce-scatter.13.cloned.1.call-done.part_ref = bf16[1000,16,128]{2,1,0:T(8,128)(2,1)} async-done(((bf16[8000,16,128]{2,1,0:T(8,128)(2,1)}), bf16[1000,16,128]{2,1,0:T(8,128)(2,1)}) %reduce-scatter.13.cloned.1.call-update) | async-done | bytes 4096016 | tf_op jit(solution)/shard_map/reduce_scatter | solution.py:504
  1955.5 8.2 join_rows.4.refs_0_
  1963.7 189.1 %reduce-scatter.11.cloned.1.call-done.part_ref = bf16[1000,16,128]{2,1,0:T(8,128)(2,1)} async-done(((bf16[8000,16,128]{2,1,0:T(8,128)(2,1)}), bf16[1000,16,128]{2,1,0:T(8,128)(2,1)}) %reduce-scatter.11.cloned.1.call-update) | async-done | bytes 4096016 | tf_op jit(solution)/shard_map/reduce_scatter | solution.py:504
  2152.8 8.2 join_rows.5.refs_0_
  2161.1 189.1 %reduce-scatter.9.cloned.1.call-done.part_ref = bf16[1000,16,128]{2,1,0:T(8,128)(2,1)} async-done(((bf16[8000,16,128]{2,1,0:T(8,128)(2,1)}), bf16[1000,16,128]{2,1,0:T(8,128)(2,1)}) %reduce-scatter.9.cloned.1.call-update) | async-done | bytes 4096016 | tf_op jit(solution)/shard_map/reduce_scatter | solution.py:504
  2350.1 8.2 join_rows.6.refs_0_
  2358.4 189.1 %reduce-scatter.7.cloned.1.call-done.part_ref = bf16[1000,16,128]{2,1,0:T(8,128)(2,1)} async-done(((bf16[8000,16,128]{2,1,0:T(8,128)(2,1)}), bf16[1000,16,128]{2,1,0:T(8,128)(2,1)}) %reduce-scatter.7.cloned.1.call-update) | async-done | bytes 4096016 | tf_op jit(solution)/shard_map/reduce_scatter | solution.py:504
  2547.4 8.2 join_rows.7
  (29 shorter events, 0.5 us)
Async XLA Ops:
  7.2 29.3 %copy-start = (s32[8,1024]{1,0:T(8,128)S(1)}, s32[8,1024]{1,0:T(8,128)}, u32[]{:S(2)}) copy-start(s32[8,1024]{1,0:T(8,128)} %param.8) | copy-start | bytes 98308
  7.2 30.0 %copy-start.2 = (bf16[256]{0:T(256)(128)(2,1)S(1)}, bf16[256]{0:T(256)(128)(2,1)}, u32[]{:S(2)}) copy-start(bf16[256]{0:T(256)(128)(2,1)} %param.10) | copy-start | bytes 1540
  7.2 103.0 %all-gather.9.cloned.1.call-start = ((), (), s32[]{:S(2)}) async-start(), calls=%async_computation.8 | async-start | bytes 9437184 | tf_op jit(solution)/shard_map/all_gather | solution.py:468
  7.9 180.6 %all-gather.7.cloned.1.call-start = ((), (), s32[]{:S(2)}) async-start(), calls=%async_computation.7 | async-start | bytes 11796480 | tf_op jit(solution)/shard_map/all_gather | solution.py:469
  10.5 683.3 %all-gather.5.cloned.1.call-start = ((), (), s32[]{:S(2)}) async-start(), calls=%async_computation.6 | async-start | bytes 147456000 | tf_op jit(solution)/shard_map/all_gather | solution.py:471
  36.5 1753.9 %reduce-scatter.17.cloned.1.call-start = ((), (), s32[]{:S(2)}) async-start(), calls=%async_computation.14 | async-start | bytes 9437184 | tf_op jit(solution)/shard_map/reduce_scatter | solution.py:514
  1582.6 210.7 %reduce-scatter.15.cloned.1.call-start = ((), (), s32[]{:S(2)}) async-start(), calls=%async_computation.13 | async-start | bytes 11796480 | tf_op jit(solution)/shard_map/reduce_scatter | solution.py:511
  1683.4 272.2 %reduce-scatter.13.cloned.1.call-start = ((), (), s32[]{:S(2)}) async-start(), calls=%async_computation.12 | async-start | bytes 36864000 | tf_op jit(solution)/shard_map/reduce_scatter | solution.py:504
  1683.9 468.9 %reduce-scatter.11.cloned.1.call-start = ((), (), s32[]{:S(2)}) async-start(), calls=%async_computation.11 | async-start | bytes 36864000 | tf_op jit(solution)/shard_map/reduce_scatter | solution.py:504
  1684.7 1.5 copy-start.1
  1684.7 665.4 %reduce-scatter.9.cloned.1.call-start = ((), (), s32[]{:S(2)}) async-start(), calls=%async_computation.10 | async-start | bytes 36864000 | tf_op jit(solution)/shard_map/reduce_scatter | solution.py:504
  1685.5 862.0 %reduce-scatter.7.cloned.1.call-start = ((), (), s32[]{:S(2)}) async-start(), calls=%async_computation.9 | async-start | bytes 36864000 | tf_op jit(solution)/shard_map/reduce_scatter | solution.py:504
Sparse Core Ops, SparseCore 0:
  9.8 51.5 all-gather.8
  63.8 59.5 all-gather.6
  125.8 567.9 all-gather.4
  1582.8 63.5 reduce-scatter.16
  1683.5 74.2 reduce-scatter.14
  1761.9 193.5 reduce-scatter.12
  1959.2 193.5 reduce-scatter.10
  2156.5 193.5 reduce-scatter.8
  2353.8 193.5 reduce-scatter.6
where the time goes:
time: 2570 us; the launch traced here: 2560 us
  waiting for transfers between devices  1230 us (48%)
  Pallas kernels  911 us (35%)
  matrix products  339 us (13%)
  blocking collectives  35.6 us (1%)
    reduce_scatter x4, waiting for transfers between devices, device_step(): lax.psum_scatter(parts[k], 'fsdp', scatter_dimension=0, tiled=True)  725 us
    all_gather x1, waiting for transfers between devices, device_step(): table = lax.all_gather(split_rows(embed_table), 'fsdp', axis=0, tiled=True)  505 us
    pallas_call x1, Pallas kernels, attention(): pl.pallas_call(functools.partial(attention_kernel, group, dim), grid=(ste...  394 us
    pallas_call x1, Pallas kernels, input_grad(): pl.pallas_call(input_grad_kernel, grid_spec=pltpu.PrefetchScalarGridSpec(...  174 us
    pallas_call x1, Pallas kernels, embed_project(): pl.pallas_call(embed_kernel, grid_spec=pltpu.PrefetchScalarGridSpec(num_s...  155 us
    dot_general x1, matrix products, device_step(): jnp.dot(draw_t, normed, preferred_element_type=F32).astype(BF16)  101 us
    pallas_call x4, Pallas kernels, table_grad(): pl.pallas_call(table_grad_kernel, grid_spec=pltpu.PrefetchScalarGridSpec(...  85.6 us
    dot_general x1, matrix products, device_step(): lax.dot_general(mixed_t, wout_full, (((0,), (0,)), ((), ())), preferred_e...  80.5 us
  transfers between devices with their start and end apart: 9, of which 5 were waited for; matrix products, arithmetic and copies ran while one was open for 11% of the time, Pallas kernels for 4%

commit v1 on v0

--- a/solution.py
+++ b/solution.py
@@ -13,6 +13,7 @@
 WINDOWS = 4
 LANES = 128
 ROWS = 256
+HALVES = 2
 PARTS = 4
 RUN = 128
 
@@ -53,7 +54,7 @@
         out_ref[:, j * LANES : (j + 1) * LANES] = wide[pl.ds(j, rows, stride=slabs), :]
 
 
-def join_rows(part, whole, index, count, scale, block=200):
+def join_rows(part, whole, half, index, scale, block=200):
     rows, slabs, _ = part.shape
     width = slabs * LANES
     steps = rows // block
@@ -67,9 +68,9 @@
     return pl.pallas_call(
         functools.partial(join_kernel, scale),
         grid=(steps,),
-        out_shape=jax.ShapeDtypeStruct((rows * count, width), F32),
+        out_shape=jax.ShapeDtypeStruct((rows * PARTS, width * HALVES), F32),
         in_specs=in_specs,
-        out_specs=pl.BlockSpec((block, width), lambda i: (index * steps + i, 0)),
+        out_specs=pl.BlockSpec((block, width), lambda i: (index * steps + i, half)),
         scratch_shapes=[pltpu.VMEM((block * slabs, LANES), F32)],
         input_output_aliases=aliases,
         cost_estimate=pl.CostEstimate(flops=rows * width, bytes_accessed=6 * rows * width, transcendentals=0),
@@ -77,7 +78,7 @@
     )(*operands)
 
 
-def embed_kernel(ids_ref, table_ref, gain_ref, weight_ref, x_ref, normed_ref, raw_ref, fetched, wide, sems):
+def embed_kernel(ids_ref, table_ref, gain_ref, weight_ref, x_ref, normed_ref, scale_ref, raw_ref, fetched, wide, sems):
     step, steps = pl.program_id(0), pl.num_programs(0)
     rows, width = x_ref.shape
     slabs = width // LANES
@@ -106,6 +107,8 @@
         square += x_part * x_part
         x_ref[:, j * LANES : (j + 1) * LANES] = x_part.astype(BF16)
     scale = lax.rsqrt(jnp.sum(square, axis=1, keepdims=True) * (1.0 / width) + NORM_EPS)
+    scale = jnp.broadcast_to(scale, (rows, LANES))
+    scale_ref[...] = scale
     for j in range(slabs):
         cols = slice(j * LANES, (j + 1) * LANES)
         normed_ref[:, cols] = (x_ref[:, cols].astype(F32) * scale * gain_ref[:, cols]).astype(BF16)
@@ -130,6 +133,7 @@
             out_specs=[
                 pl.BlockSpec((ROWS, width), lambda i, ids: (i, 0)),
                 pl.BlockSpec((ROWS, width), lambda i, ids: (i, 0)),
+                pl.BlockSpec((ROWS, LANES), lambda i, ids: (i, 0)),
                 pl.BlockSpec((1, features, ROWS), lambda i, ids: (i, 0, 0)),
             ],
             scratch_shapes=[
@@ -141,6 +145,7 @@
         out_shape=[
             jax.ShapeDtypeStruct((tokens, width), BF16),
             jax.ShapeDtypeStruct((tokens, width), BF16),
+            jax.ShapeDtypeStruct((tokens, LANES), F32),
             jax.ShapeDtypeStruct((steps, features, ROWS), F32),
         ],
         cost_estimate=pl.CostEstimate(flops=2 * tokens * width * features, bytes_accessed=tokens * (6 * width + 4 * features), transcendentals=tokens),
@@ -169,92 +174,121 @@
     return scale * (grads - unit * jnp.mean(unit * grads, axis=0, keepdims=True))
 
 
-def attention_kernel(group, dim, raw_ref, dmix_ref, cos_ref, sin_ref, mix_ref, draw_ref):
+def softmax_and_grad(scores, d_probs, causal, empty):
+    half = scores.shape[0] // 2
+    early = jnp.where(causal, jnp.exp(scores[:half, :half]), 0.0)
+    cross = jnp.exp(scores[:half, half:])
+    late = jnp.where(causal, jnp.exp(scores[half:, half:]), 0.0)
+    early_inv = 1.0 / jnp.sum(early, axis=0, keepdims=True)
+    late_inv = 1.0 / jnp.sum(cross + late, axis=0, keepdims=True)
+    early, cross, late = early * early_inv, cross * late_inv, late * late_inv
+    probs = jnp.concatenate(
+        [
+            jnp.concatenate([early.astype(BF16), cross.astype(BF16)], axis=1),
+            jnp.concatenate([empty, late.astype(BF16)], axis=1),
+        ],
+        axis=0,
+    )
+    d_early, d_cross, d_late = d_probs[:half, :half], d_probs[:half, half:], d_probs[half:, half:]
+    early_dot = jnp.sum(early * d_early, axis=0, keepdims=True)
+    late_dot = jnp.sum(cross * d_cross + late * d_late, axis=0, keepdims=True)
+    d_scores = jnp.concatenate(
+        [
+            jnp.concatenate([(early * (d_early - early_dot)).astype(BF16), (cross * (d_cross - late_dot)).astype(BF16)], axis=1),
+            jnp.concatenate([empty, (late * (d_late - late_dot)).astype(BF16)], axis=1),
+        ],
+        axis=0,
+    )
+    return probs, d_scores
+
+
+def attention_kernel(kv_heads, group, dim, raw_ref, dmix_ref, cos_ref, sin_ref, mix_ref, draw_ref, pull_ref):
     tokens = raw_ref.shape[2]
     half = tokens // 2
+    block = (group + 2) * dim
     cosine, sine = cos_ref[...], sin_ref[...]
-    k_unit, k_scale = head_norm(rotate(raw_ref[0, group * dim : (group + 1) * dim, :], cosine, sine))
-    key_t = k_unit.astype(BF16)
-    key_f = key_t.astype(F32) * dim**-0.5
-    key_small_t = key_f.astype(BF16)
-    key_small = key_f.T.astype(BF16)
-    value_f = raw_ref[0, (group + 1) * dim : (group + 2) * dim, :].astype(BF16)
-    value_t = value_f
-    value = value_f.astype(F32).T.astype(BF16)
     keys_at = lax.broadcasted_iota(jnp.int32, (half, half), 0)
     queries_at = lax.broadcasted_iota(jnp.int32, (half, half), 1)
     causal = queries_at >= keys_at
     empty = jnp.zeros((half, half), BF16)
-    d_key = jnp.zeros((dim, tokens), F32)
-    d_value = jnp.zeros((dim, tokens), F32)
-    for head in range(group):
-        rows = slice(head * dim, (head + 1) * dim)
-        q_unit, q_scale = head_norm(rotate(raw_ref[0, rows, :], cosine, sine))
-        query_t = q_unit.astype(BF16)
-        d_out = dmix_ref[rows, :]
-        scores = jnp.dot(key_small, query_t, preferred_element_type=F32)
-        d_probs = jnp.dot(value, d_out, preferred_element_type=F32)
-        early = jnp.where(causal, jnp.exp(scores[:half, :half]), 0.0)
-        cross = jnp.exp(scores[:half, half:])
-        late = jnp.where(causal, jnp.exp(scores[half:, half:]), 0.0)
-        early_inv = 1.0 / jnp.sum(early, axis=0, keepdims=True)
-        late_inv = 1.0 / (jnp.sum(cross, axis=0, keepdims=True) + jnp.sum(late, axis=0, keepdims=True))
-        early, cross, late = early * early_inv, cross * late_inv, late * late_inv
-        probs = jnp.concatenate(
-            [
-                jnp.concatenate([early.astype(BF16), cross.astype(BF16)], axis=1),
-                jnp.concatenate([empty, late.astype(BF16)], axis=1),
-            ],
-            axis=0,
-        )
-        mix_ref[rows, :] = jnp.dot(value_t, probs, preferred_element_type=F32).astype(BF16)
-        d_early, d_cross, d_late = d_probs[:half, :half], d_probs[:half, half:], d_probs[half:, half:]
-        early_dot = jnp.sum(early * d_early, axis=0, keepdims=True)
-        late_dot = jnp.sum(cross * d_cross, axis=0, keepdims=True) + jnp.sum(late * d_late, axis=0, keepdims=True)
-        d_scores = jnp.concatenate(
-            [
-                jnp.concatenate([(early * (d_early - early_dot)).astype(BF16), (cross * (d_cross - late_dot)).astype(BF16)], axis=1),
-                jnp.concatenate([empty, (late * (d_late - late_dot)).astype(BF16)], axis=1),
-            ],
-            axis=0,
-        )
-        d_query = jnp.dot(key_small_t, d_scores, preferred_element_type=F32)
-        d_key += lax.dot_general(query_t, d_scores, NT, preferred_element_type=F32)
-        d_value += lax.dot_general(d_out, probs, NT, preferred_element_type=F32)
-        draw_ref[rows, :] = rotate_back(head_norm_back(d_query, q_unit, q_scale), cosine, sine).astype(BF16)
-    d_key = rotate_back(head_norm_back(d_key * dim**-0.5, k_unit, k_scale), cosine, sine)
-    draw_ref[group * dim : (group + 1) * dim, :] = d_key.astype(BF16)
-    draw_ref[(group + 1) * dim :, :] = d_value.astype(BF16)
+
+    def one_kv_head(kv, pull):
+        def rows(at):
+            return pl.ds(pl.multiple_of(kv * block + at * dim, dim), dim)
+
+        def mixed_rows(head):
+            return pl.ds(pl.multiple_of((kv * group + head) * dim, dim), dim)
+
+        def put(at, values):
+            values = values.astype(BF16)
+            draw_ref[rows(at), :] = values
+            return values.astype(F32) * raw_ref[0, rows(at), :]
+
+        k_unit, k_scale = head_norm(rotate(raw_ref[0, rows(group), :], cosine, sine))
+        key_f = k_unit.astype(BF16).astype(F32) * dim**-0.5
+        key_small_t = key_f.astype(BF16)
+        key_small = key_f.T.astype(BF16)
+        value_t = raw_ref[0, rows(group + 1), :].astype(BF16)
+        value = value_t.astype(F32).T.astype(BF16)
+        d_key = jnp.zeros((dim, tokens), F32)
+        d_value = jnp.zeros((dim, tokens), F32)
+
+        def begin(head):
+            q_unit, q_scale = head_norm(rotate(raw_ref[0, rows(head), :], cosine, sine))
+            query_t = q_unit.astype(BF16)
+            d_out = dmix_ref[mixed_rows(head), :]
+            scores = jnp.dot(key_small, query_t, preferred_element_type=F32)
+            d_probs = jnp.dot(value, d_out, preferred_element_type=F32)
+            return q_unit, q_scale, query_t, d_out, scores, d_probs
+
+        ahead = begin(0)
+        for head in range(group):
+            q_unit, q_scale, query_t, d_out, scores, d_probs = ahead
+            if head + 1 < group:
+                ahead = begin(head + 1)
+            probs, d_scores = softmax_and_grad(scores, d_probs, causal, empty)
+            mix_ref[mixed_rows(head), :] = jnp.dot(value_t, probs, preferred_element_type=F32).astype(BF16)
+            d_query = jnp.dot(key_small_t, d_scores, preferred_element_type=F32)
+            d_key += lax.dot_general(query_t, d_scores, NT, preferred_element_type=F32)
+            d_value += lax.dot_general(d_out, probs, NT, preferred_element_type=F32)
+            pull += put(head, rotate_back(head_norm_back(d_query, q_unit, q_scale), cosine, sine))
+        pull += put(group, rotate_back(head_norm_back(d_key * dim**-0.5, k_unit, k_scale), cosine, sine))
+        return pull + put(group + 1, d_value)
+
+    pull = lax.fori_loop(0, kv_heads, one_kv_head, jnp.zeros((dim, tokens), F32))
+    pull = jnp.sum(pull, axis=0, keepdims=True)
+    pull_ref[...] = jnp.broadcast_to(pull, (LANES, tokens)).T
 
 
 def attention(raw, d_mixed_t, cosine, sine, kv_heads, group, dim):
     steps, features, tokens = raw.shape
-    block = features // kv_heads
-    width = group * dim
+    width = kv_heads * group * dim
     pairs = steps * kv_heads * group * tokens * tokens
     return pl.pallas_call(
-        functools.partial(attention_kernel, group, dim),
-        grid=(steps, kv_heads),
+        functools.partial(attention_kernel, kv_heads, group, dim),
+        grid=(steps,),
         in_specs=[
-            pl.BlockSpec((1, block, tokens), lambda w, k: (w, k, 0)),
-            pl.BlockSpec((width, tokens), lambda w, k: (k, w)),
-            pl.BlockSpec((dim // 2, tokens), lambda w, k: (0, w % WINDOWS)),
-            pl.BlockSpec((dim // 2, tokens), lambda w, k: (0, w % WINDOWS)),
+            pl.BlockSpec((1, features, tokens), lambda w: (w, 0, 0)),
+            pl.BlockSpec((width, tokens), lambda w: (0, w)),
+            pl.BlockSpec((dim // 2, tokens), lambda w: (0, w % WINDOWS)),
+            pl.BlockSpec((dim // 2, tokens), lambda w: (0, w % WINDOWS)),
         ],
         out_specs=[
-            pl.BlockSpec((width, tokens), lambda w, k: (k, w)),
-            pl.BlockSpec((block, tokens), lambda w, k: (k, w)),
+            pl.BlockSpec((width, tokens), lambda w: (0, w)),
+            pl.BlockSpec((features, tokens), lambda w: (0, w)),
+            pl.BlockSpec((tokens, LANES), lambda w: (w, 0)),
         ],
         out_shape=[
-            jax.ShapeDtypeStruct((width * kv_heads, steps * tokens), BF16),
+            jax.ShapeDtypeStruct((width, steps * tokens), BF16),
             jax.ShapeDtypeStruct((features, steps * tokens), BF16),
+            jax.ShapeDtypeStruct((steps * tokens, LANES), F32),
         ],
         cost_estimate=pl.CostEstimate(flops=12 * pairs * dim, bytes_accessed=8 * raw.size, transcendentals=pairs),
         name='attention',
     )(raw, d_mixed_t, cosine, sine)
 
 
-def input_grad_kernel(place_ref, draw_ref, weight_ref, x_ref, dh_ref, gain_ref, sorted_ref, dgain_ref, d_normed, wide, sems):
+def input_grad_kernel(depth, place_ref, draw_ref, weight_ref, x_ref, dh_ref, gain_ref, scale_ref, pull_ref, sorted_ref, dgain_ref, d_normed, wide, sems):
     step, steps = pl.program_id(0), pl.num_programs(0)
     rows, width = x_ref.shape
     slabs = width // LANES
@@ -264,15 +298,8 @@
         pltpu.make_async_copy(wide.at[which], sorted_ref.at[pl.ds(0, rows * slabs)], sems.at[which]).wait()
 
     d_normed[...] = jnp.dot(draw_ref[...].T, weight_ref[...], preferred_element_type=F32)
-    square = jnp.zeros((rows, LANES), F32)
-    cross = jnp.zeros((rows, LANES), F32)
-    for j in range(slabs):
-        cols = slice(j * LANES, (j + 1) * LANES)
-        x_part = x_ref[:, cols].astype(F32)
-        square += x_part * x_part
-        cross += x_part * d_normed[:, cols] * gain_ref[:, cols]
-    scale = lax.rsqrt(jnp.sum(square, axis=1, keepdims=True) * (1.0 / width) + NORM_EPS)
-    pull = jnp.sum(cross, axis=1, keepdims=True) * (1.0 / width) * scale * scale
+    scale = scale_ref[...]
+    pull = pull_ref[...] * scale * (1.0 / depth)
 
     @pl.when(step == 0)
     def _():
@@ -305,22 +332,25 @@
         drain(slot)
 
 
-def input_grad(place, draw_t, weight_t, x, dh, gain, spare):
-    tokens, width = x.shape
+def input_grad(place, draw_t, weight_t, x, dh, gain, scale, pull, half, spare):
+    tokens, depth = x.shape
+    width = depth // HALVES
     slabs = width // LANES
     features = draw_t.shape[0]
     steps = tokens // ROWS
     return pl.pallas_call(
-        input_grad_kernel,
+        functools.partial(input_grad_kernel, depth),
         grid_spec=pltpu.PrefetchScalarGridSpec(
             num_scalar_prefetch=1,
             grid=(steps,),
             in_specs=[
                 pl.BlockSpec((features, ROWS), lambda i, place: (0, i)),
-                pl.BlockSpec((features, width), lambda i, place: (0, 0)),
-                pl.BlockSpec((ROWS, width), lambda i, place: (i, 0)),
-                pl.BlockSpec((ROWS, width), lambda i, place: (i, 0)),
-                pl.BlockSpec((1, width), lambda i, place: (0, 0)),
+                pl.BlockSpec((features, width), lambda i, place: (0, half)),
+                pl.BlockSpec((ROWS, width), lambda i, place: (i, half)),
+                pl.BlockSpec((ROWS, width), lambda i, place: (i, half)),
+                pl.BlockSpec((1, width), lambda i, place: (0, half)),
+                pl.BlockSpec((ROWS, LANES), lambda i, place: (i, 0)),
+                pl.BlockSpec((ROWS, LANES), lambda i, place: (i, 0)),
             ],
             out_specs=[
                 pl.BlockSpec(memory_space=pl.ANY),
@@ -336,9 +366,9 @@
             jax.ShapeDtypeStruct(((tokens + spare) * slabs, LANES), F32),
             jax.ShapeDtypeStruct((8, width), F32),
         ],
-        cost_estimate=pl.CostEstimate(flops=2 * tokens * width * features, bytes_accessed=tokens * (8 * width + 2 * features), transcendentals=tokens),
+        cost_estimate=pl.CostEstimate(flops=2 * tokens * width * features, bytes_accessed=tokens * (8 * width + 2 * features), transcendentals=0),
         name='input_grad',
-    )(place, draw_t, weight_t, x, dh, gain)
+    )(place, draw_t, weight_t, x, dh, gain, scale, pull)
 
 
 def table_grad_kernel(bounds_ref, same_ref, target_ref, sorted_ref, zero_ref, out_ref, fetched, summed, in_sems, out_sems):
@@ -424,6 +454,68 @@
     )(bounds, same, target, sorted_rows, zero_part)
 
 
+def pair_sum_kernel(part_ref, out_ref, came, mine, send_sems, recv_sems, in_sems, out_sems):
+    chips, rows = came.shape[:2]
+    me = lax.axis_index('fsdp')
+    core = lax.rem(me, 2)
+    partner = me + 1 - 2 * core
+    barrier = pltpu.get_barrier_semaphore()
+    pl.semaphore_signal(barrier, inc=1, device_id=(partner,), device_id_type=pl.DeviceIdType.MESH)
+    pl.semaphore_wait(barrier, 1)
+    sends, loads, stores = [], [], []
+    for q in range(chips):
+        sends.append(
+            pltpu.make_async_remote_copy(
+                src_ref=part_ref.at[pl.ds((2 * q + 1 - core) * rows, rows)],
+                dst_ref=came.at[q],
+                send_sem=send_sems.at[q],
+                recv_sem=recv_sems.at[q],
+                device_id=(partner,),
+                device_id_type=pl.DeviceIdType.MESH,
+            )
+        )
+        loads.append(pltpu.make_async_copy(part_ref.at[pl.ds((2 * q + core) * rows, rows)], mine.at[q], in_sems.at[q]))
+        stores.append(pltpu.make_async_copy(mine.at[q], out_ref.at[pl.ds(q * rows, rows)], out_sems.at[q]))
+        sends[q].start()
+        loads[q].start()
+    for q in range(chips):
+        loads[q].wait()
+        sends[q].wait_recv()
+
+        def add(i, carry):
+            at = pl.ds(i * 8, 8)
+            mine[q, at] = (mine[q, at].astype(F32) + came[q, at].astype(F32)).astype(BF16)
+            return carry
+
+        lax.fori_loop(0, rows // 8, add, 0)
+        stores[q].start()
+    for q in range(chips):
+        stores[q].wait()
+        sends[q].wait_send()
+
+
+def pair_sum(part, index, devices):
+    total, slabs, _ = part.shape
+    chips, rows = devices // 2, total // devices
+    return pl.pallas_call(
+        pair_sum_kernel,
+        out_shape=jax.ShapeDtypeStruct((chips * rows, slabs, LANES), BF16),
+        in_specs=[pl.BlockSpec(memory_space=pl.ANY)],
+        out_specs=pl.BlockSpec(memory_space=pl.ANY),
+        scratch_shapes=[
+            pltpu.VMEM((chips, rows, slabs, LANES), BF16),
+            pltpu.VMEM((chips, rows, slabs, LANES), BF16),
+            pltpu.SemaphoreType.DMA((chips,)),
+            pltpu.SemaphoreType.DMA((chips,)),
+            pltpu.SemaphoreType.DMA((chips,)),
+            pltpu.SemaphoreType.DMA((chips,)),
+        ],
+        compiler_params=pltpu.CompilerParams(collective_id=index),
+        cost_estimate=pl.CostEstimate(flops=part.size, bytes_accessed=4 * part.size, transcendentals=0),
+        name='pair_sum',
+    )(part)
+
+
 def zero_kernel(*refs):
     *out_refs, block, sem = refs
     block[...] = jnp.zeros_like(block)
@@ -492,21 +584,30 @@
         cosine, sine = jnp.cos(angles), jnp.sin(angles)
 
         d_mixed_t = lax.dot_general(wout_full, dh, NT, preferred_element_type=F32).astype(BF16)
-        zero_parts = zero_tables(PARTS, part_rows, slabs)
+        half_slabs = slabs // HALVES
+        zero_parts = zero_tables(PARTS * HALVES, part_rows, half_slabs)
         d_mixed_t, *zero_parts = lax.optimization_barrier((d_mixed_t, *zero_parts))
 
-        x, normed, raw = embed_project(ids, table, gain, weight_t)
-        mixed_t, draw_t = attention(raw, d_mixed_t, cosine, sine, kv_heads, group, dim)
-        sorted_rows, dgain = input_grad(place, draw_t, weight_t, x, dh, gain, RUN)
-        parts = [table_grad(bounds[k : k + 2], same, target, sorted_rows, zero_parts[k]) for k in range(PARTS)]
-        shares = []
-        for k in range(PARTS):
-            shares.append(lax.psum_scatter(parts[k], 'fsdp', scatter_dimension=0, tiled=True))
+        x, normed, scale, raw = embed_project(ids, table, gain, weight_t)
+        mixed_t, draw_t, pull = attention(raw, d_mixed_t, cosine, sine, kv_heads, group, dim)
+        same_core = [list(range(core, devices, 2)) for core in range(2)]
+        dgains, shares, sums = [], [], []
+        for h in range(HALVES):
+            if sums:
+                pull, *_ = lax.optimization_barrier((pull, *sums))
+            sorted_rows, dgain = input_grad(place, draw_t, weight_t, x, dh, gain, scale, pull, h, RUN)
+            dgains.append(jnp.sum(dgain, axis=0))
+            for k in range(PARTS):
+                index = h * PARTS + k
+                part = table_grad(bounds[k : k + 2], same, target, sorted_rows, zero_parts[index])
+                sums.append(pair_sum(part, index, devices))
+                shares.append(lax.psum_scatter(sums[-1], 'fsdp', scatter_dimension=0, tiled=True, axis_index_groups=same_core))
         grad_table = None
-        for k in range(PARTS):
-            grad_table = join_rows(shares[k], grad_table, k, PARTS, 1.0 / devices)
-
-        mixed_t, draw_t, *_ = lax.optimization_barrier((mixed_t, draw_t, *parts))
+        for h in range(HALVES):
+            for k in range(PARTS):
+                grad_table = join_rows(shares[h * PARTS + k], grad_table, h, k, 1.0 / devices)
+
+        mixed_t, draw_t, *_ = lax.optimization_barrier((mixed_t, draw_t, *sums))
         grad_weight = jnp.dot(draw_t, normed, preferred_element_type=F32).astype(BF16)
         grad_weight = lax.psum_scatter(grad_weight, 'fsdp', scatter_dimension=1, tiled=True)
         grad_weight = grad_weight.astype(F32) / devices
@@ -515,7 +616,7 @@
         grad_wout = grad_wout.astype(F32) / devices
         hidden = x.astype(F32) + lax.dot_general(mixed_t, wout_full, (((0,), (0,)), ((), ())), preferred_element_type=F32)
         hidden = hidden.astype(BF16).reshape(batch, seq_len, width)
-        grad_gain = lax.psum_scatter(jnp.sum(dgain, axis=0), 'fsdp', scatter_dimension=0, tiled=True) / devices
+        grad_gain = lax.psum_scatter(jnp.concatenate(dgains), 'fsdp', scatter_dimension=0, tiled=True) / devices
 
         grad_weight = grad_weight.reshape(kv_heads, (group + 2) * dim, -1)
 

time: 2570 us -> 2520 us (0.981)
  waiting for transfers between devices: 1230 us -> 1090 us
  Pallas kernels: 911 us -> 998 us
    reduce_scatter x4 -> x8, waiting for transfers between devices: 725 us -> 579 us  [device_step(): lax.psum_scatter(sums[-1], 'fsdp', scatter_dimension=0, tiled=True, axis_...]
    pallas_call x4 -> x8, Pallas kernels: 85.6 us -> 157 us  [table_grad(): pl.pallas_call(table_grad_kernel, grid_spec=pltpu.PrefetchScalarGridSpec(...]
    pallas_call x2 -> x11, Pallas kernels: 568 us -> 575 us  [the longest x1 256 us: attention(): pl.pallas_call(functools.partial(attention_kernel, kv_heads, group, dim),...]
  transfers between devices with their start and end apart: 9 -> 13, of which waited for: 5 -> 9; matrix products, arithmetic and copies ran while one was open for 11% -> 11% of each run, Pallas kernels for 4% -> 4%
where the time goes in v1:
time: 2520 us; the launch traced here: 2510 us
  waiting for transfers between devices  1090 us (43%)
  Pallas kernels  998 us (40%)
  matrix products  339 us (13%)
  blocking collectives  35.2 us (1%)
    reduce_scatter x8, waiting for transfers between devices, device_step(): lax.psum_scatter(sums[-1], 'fsdp', scatter_dimension=0, tiled=True, axis_...  579 us
    all_gather x1, waiting for transfers between devices, device_step(): table = lax.all_gather(split_rows(embed_table), 'fsdp', axis=0, tiled=True)  505 us
    pallas_call x1, Pallas kernels, attention(): pl.pallas_call(functools.partial(attention_kernel, kv_heads, group, dim),...  256 us
    pallas_call x2, Pallas kernels, input_grad(): pl.pallas_call(functools.partial(input_grad_kernel, depth), grid_spec=plt...  193 us
    pallas_call x8, Pallas kernels, table_grad(): pl.pallas_call(table_grad_kernel, grid_spec=pltpu.PrefetchScalarGridSpec(...  157 us
    pallas_call x1, Pallas kernels, embed_project(): pl.pallas_call(embed_kernel, grid_spec=pltpu.PrefetchScalarGridSpec(num_s...  155 us
    pallas_call x8, Pallas kernels, pair_sum(): pl.pallas_call(pair_sum_kernel, out_shape=jax.ShapeDtypeStruct((chips * r...  126 us
    dot_general x1, matrix products, device_step(): jnp.dot(draw_t, normed, preferred_element_type=F32).astype(BF16)  101 us
  transfers between devices with their start and end apart: 13, of which 9 were waited for; matrix products, arithmetic and copies ran while one was open for 11% of the time, Pallas kernels for 4%

profile of v1, /device:TPU:0, one launch (start us, length us, event | category | flops | bytes accessed | tf_op | source)
XLA Modules:
  0.0 2506.1 jit_solution(16351476204463107188)
XLA Ops:
  10.5 25.9 %split_rows.1 = bf16[4000,16,128]{2,1,0:T(8,128)(2,1)} custom-call(bf16[4000,2048]{1,0:T(8,128)(2,1)} %table_ref.1), custom_call_target="tpu_custom_call" | custom-call | flops 8192000 | bytes 32768000 | tf_op jit(solution)/shard_map/split_rows/pallas_call | solution.py:36
  37.8 12.6 all-gather
  51.1 6.2 sort.30
  58.1 6.8 sort.31
  64.9 43.0 %zero_tables.1 = (bf16[8000,8,128]{2,1,0:T(8,128)(2,1)}, bf16[8000,8,128]{2,1,0:T(8,128)(2,1)}, bf16[8000,8,128]{2,1,0:T(8,128)(2,1)}, bf16[8000,8,128]{2,1,0:T(...) custom-call(), custom_call_target="tpu_custom_call" | custom-call | flops 65536000 | bytes 131072000 | tf_op jit(solution)/shard_map/zero_tables/pallas_call | solution.py:531
  110.8 78.3 %convolution_convert_fusion.dmix_ref = bf16[2048,8192]{1,0:T(8,128)(2,1)} fusion(bf16[2048,2048]{1,0:T(8,128)(2,1)} %all-gather.9.cloned.1.call-done, bf16[8192,2048]{1,0:T(8,128)(2,1)} %bitcast.43), kind=kOutput, calls=%fused_computation.1 | convolution fusion | flops 68736253952 | bytes 75497472 | tf_op jit(solution)/shard_map/dot_general | solution.py:586
  189.0 505.4 %all-gather.5.cloned.1.call-done.table_ref = bf16[32000,16,128]{2,1,0:T(8,128)(2,1)} async-done(((bf16[4000,16,128]{2,1,0:T(8,128)(2,1)}), bf16[32000,16,128]{2,1,0:T(8,128)(2,1)}) %all-gather.5.cloned.1.call-update) | async-done | bytes 131072016 | tf_op jit(solution)/shard_map/all_gather | solution.py:563
  694.4 155.4 %embed_project.1 = (bf16[8192,2048]{1,0:T(8,128)(2,1)}, bf16[8192,2048]{1,0:T(8,128)(2,1)}, f32[8192,128]{1,0:T(8,128)}, f32[32,2560,256]{2,1,0:T(8,128)}) custom-call(s32[8192]{0:T(1024)} %bitcast.41, bf16[32000,16,128]{2,1,0:T(8,128)(2,1)} %all-gather.5.cloned.1.call-done.table_ref, f32[1,2048]{1,0:T(1,128)} %convert.3.gain_ref, ...), custom_call_target="tpu_custom_call" | custom-call | flops 85899345920 | bytes 184549376 | tf_op jit(solution)/shard_map/embed_project/pallas_call | solution.py:123
  849.8 255.9 %attention.1 = (bf16[2048,8192]{1,0:T(8,128)(2,1)}, bf16[2560,8192]{1,0:T(8,128)(2,1)}, f32[8192,128]{1,0:T(8,128)}) custom-call(f32[32,2560,256]{2,1,0:T(8,128)} %get-tuple-element.42.raw_ref, bf16[2048,8192]{1,0:T(8,128)(2,1)} %convolution_convert_fusion.dmix_ref, f32[32,1024]{1,0:T(8,128)} %get-tuple-element.84.cos_ref, f32[32,1024]{1,0:T(8,128)} %get-tuple-element.83.sin_ref), custom_call_target="tpu_custom_call" | custom-call | flops 51539607552 | bytes 167772160 | tf_op jit(solution)/shard_map/attention/pallas_call | solution.py:267
  1105.8 96.1 %input_grad.2 = (f32[66560,128]{1,0:T(8,128)}, f32[8,1024]{1,0:T(8,128)}) custom-call(s32[8192]{0:T(1024)} %get-tuple-element.56.place_ref, bf16[2560,8192]{1,0:T(8,128)(2,1)} %get-tuple-element.73.draw_ref, bf16[2560,2048]{1,0:T(8,128)(2,1)} %all-gather.7.cloned.1.call-done.weight_ref, bf16[8192,2048]{1,0:T(8,128)(2,1)} %get-tuple-element.41.x_ref, ...), custom_call_target="tpu_custom_call" | custom-call | flops 42949672960 | bytes 109051904 | tf_op jit(solution)/shard_map/input_grad/pallas_call | solution.py:341
  1201.9 20.3 table_grad.8.part_ref
  1222.2 16.0 pair_sum.8
  1238.3 20.9 table_grad.9.part_ref
  1259.2 15.6 pair_sum.9
  1274.8 19.2 table_grad.10.part_ref
  1294.0 15.9 pair_sum.10
  1309.9 18.1 table_grad.11.part_ref
  1328.0 15.6 pair_sum.11
  1343.6 97.1 %input_grad.3 = (f32[66560,128]{1,0:T(8,128)}, f32[8,1024]{1,0:T(8,128)}) custom-call(s32[8192]{0:T(1024)} %get-tuple-element.56.place_ref, bf16[2560,8192]{1,0:T(8,128)(2,1)} %get-tuple-element.73.draw_ref, bf16[2560,2048]{1,0:T(8,128)(2,1)} %all-gather.7.cloned.1.call-done.weight_ref, bf16[8192,2048]{1,0:T(8,128)(2,1)} %get-tuple-element.41.x_ref, ...), custom_call_target="tpu_custom_call" | custom-call | flops 42949672960 | bytes 109051904 | tf_op jit(solution)/shard_map/input_grad/pallas_call | solution.py:341
  1440.8 20.3 table_grad.12.part_ref
  1461.1 16.2 pair_sum.12
  1477.3 20.9 table_grad.13.part_ref
  1498.2 15.6 pair_sum.13
  1513.8 19.2 table_grad.14.part_ref
  1533.0 15.8 pair_sum.14
  1548.8 18.1 table_grad.15.part_ref
  1567.0 15.6 pair_sum.15
  1582.5 79.2 %convolution_convert_fusion.2 = bf16[2048,2048]{1,0:T(8,128)(2,1)} fusion(bf16[2048,8192]{1,0:T(8,128)(2,1)} %get-tuple-element.70, bf16[8192,2048]{1,0:T(8,128)(2,1)} %bitcast.46), kind=kOutput, calls=%fused_computation.3 | convolution fusion | flops 68723671040 | bytes 75497472 | tf_op jit(solution)/shard_map/dot_general | solution.py:614
  1661.8 101.1 %convolution_convert_fusion.1 = bf16[2560,2048]{1,0:T(8,128)(2,1)} fusion(bf16[2560,8192]{1,0:T(8,128)(2,1)} %get-tuple-element.73.draw_ref, bf16[8192,2048]{1,0:T(8,128)(2,1)} %get-tuple-element.74), kind=kOutput, calls=%fused_computation.2 | convolution fusion | flops 85904588800 | bytes 85983232 | tf_op jit(solution)/shard_map/dot_general | solution.py:611
  1768.5 22.6 all-reduce.2
  1791.7 80.3 %add_convert_fusion = bf16[8192,2048]{1,0:T(8,128)(2,1)} fusion(bf16[8192,2048]{1,0:T(8,128)(2,1)} %get-tuple-element.41.x_ref, bf16[2048,8192]{1,0:T(8,128)(2,1)} %get-tuple-element.70, bf16[2048,2048]{1,0:T(8,128)(2,1)} %all-gather.9.cloned.1.call-done), kind=kOutput, calls=%fused_computation | convolution fusion | flops 68769808384 | bytes 109051904 | tf_op jit(solution)/shard_map/dot_general | solution.py:617
  1872.0 2.8 convert_multiply_fusion.1
  1878.6 39.7 %reduce-scatter.25.cloned.1.call-done.part_ref = bf16[1000,8,128]{2,1,0:T(8,128)(2,1)} async-done(((bf16[4000,8,128]{2,1,0:T(8,128)(2,1)}), bf16[1000,8,128]{2,1,0:T(8,128)(2,1)}) %reduce-scatter.25.cloned.1.call-update) | async-done | bytes 2048016 | tf_op jit(solution)/shard_map/reduce_scatter | solution.py:604
  1918.2 5.2 join_rows.8.refs_0_
  1923.4 77.1 %reduce-scatter.23.cloned.1.call-done.part_ref = bf16[1000,8,128]{2,1,0:T(8,128)(2,1)} async-done(((bf16[4000,8,128]{2,1,0:T(8,128)(2,1)}), bf16[1000,8,128]{2,1,0:T(8,128)(2,1)}) %reduce-scatter.23.cloned.1.call-update) | async-done | bytes 2048016 | tf_op jit(solution)/shard_map/reduce_scatter | solution.py:604
  2000.6 5.2 join_rows.9.refs_0_
  2005.8 77.1 %reduce-scatter.21.cloned.1.call-done.part_ref = bf16[1000,8,128]{2,1,0:T(8,128)(2,1)} async-done(((bf16[4000,8,128]{2,1,0:T(8,128)(2,1)}), bf16[1000,8,128]{2,1,0:T(8,128)(2,1)}) %reduce-scatter.21.cloned.1.call-update) | async-done | bytes 2048016 | tf_op jit(solution)/shard_map/reduce_scatter | solution.py:604
  2082.9 5.2 join_rows.10.refs_0_
  2088.1 77.1 %reduce-scatter.19.cloned.1.call-done.part_ref = bf16[1000,8,128]{2,1,0:T(8,128)(2,1)} async-done(((bf16[4000,8,128]{2,1,0:T(8,128)(2,1)}), bf16[1000,8,128]{2,1,0:T(8,128)(2,1)}) %reduce-scatter.19.cloned.1.call-update) | async-done | bytes 2048016 | tf_op jit(solution)/shard_map/reduce_scatter | solution.py:604
  2165.2 5.2 join_rows.11.refs_0_
  2170.4 76.9 %reduce-scatter.17.cloned.1.call-done.part_ref = bf16[1000,8,128]{2,1,0:T(8,128)(2,1)} async-done(((bf16[4000,8,128]{2,1,0:T(8,128)(2,1)}), bf16[1000,8,128]{2,1,0:T(8,128)(2,1)}) %reduce-scatter.17.cloned.1.call-update) | async-done | bytes 2048016 | tf_op jit(solution)/shard_map/reduce_scatter | solution.py:604
  2247.4 5.2 join_rows.12.refs_0_
  2252.6 77.1 %reduce-scatter.15.cloned.1.call-done.part_ref = bf16[1000,8,128]{2,1,0:T(8,128)(2,1)} async-done(((bf16[4000,8,128]{2,1,0:T(8,128)(2,1)}), bf16[1000,8,128]{2,1,0:T(8,128)(2,1)}) %reduce-scatter.15.cloned.1.call-update) | async-done | bytes 2048016 | tf_op jit(solution)/shard_map/reduce_scatter | solution.py:604
  2329.7 5.2 join_rows.13.refs_0_
  2334.9 77.0 %reduce-scatter.13.cloned.1.call-done.part_ref = bf16[1000,8,128]{2,1,0:T(8,128)(2,1)} async-done(((bf16[4000,8,128]{2,1,0:T(8,128)(2,1)}), bf16[1000,8,128]{2,1,0:T(8,128)(2,1)}) %reduce-scatter.13.cloned.1.call-update) | async-done | bytes 2048016 | tf_op jit(solution)/shard_map/reduce_scatter | solution.py:604
  2411.9 5.2 join_rows.14.refs_0_
  2417.1 77.1 %reduce-scatter.11.cloned.1.call-done.part_ref = bf16[1000,8,128]{2,1,0:T(8,128)(2,1)} async-done(((bf16[4000,8,128]{2,1,0:T(8,128)(2,1)}), bf16[1000,8,128]{2,1,0:T(8,128)(2,1)}) %reduce-scatter.11.cloned.1.call-update) | async-done | bytes 2048016 | tf_op jit(solution)/shard_map/reduce_scatter | solution.py:604
  2494.2 5.2 join_rows.15
  (62 shorter events, 19.0 us)
Async XLA Ops:
  7.2 103.6 %all-gather.9.cloned.1.call-start = ((), (), s32[]{:S(2)}) async-start(), calls=%async_computation.12 | async-start | bytes 9437184 | tf_op jit(solution)/shard_map/all_gather | solution.py:560
  7.9 181.1 %all-gather.7.cloned.1.call-start = ((), (), s32[]{:S(2)}) async-start(), calls=%async_computation.11 | async-start | bytes 11796480 | tf_op jit(solution)/shard_map/all_gather | solution.py:561
  10.5 684.0 %all-gather.5.cloned.1.call-start = ((), (), s32[]{:S(2)}) async-start(), calls=%async_computation.10 | async-start | bytes 147456000 | tf_op jit(solution)/shard_map/all_gather | solution.py:563
  36.4 0.8 copy-start
  36.4 1.4 copy-start.3
  36.4 1835.5 %reduce-scatter.29.cloned.1.call-start = ((), (), s32[]{:S(2)}) async-start(), calls=%async_computation.22 | async-start | bytes 9437184 | tf_op jit(solution)/shard_map/reduce_scatter | solution.py:615
  1661.8 213.0 %reduce-scatter.27.cloned.1.call-start = ((), (), s32[]{:S(2)}) async-start(), calls=%async_computation.21 | async-start | bytes 11796480 | tf_op jit(solution)/shard_map/reduce_scatter | solution.py:612
  1762.9 155.3 %reduce-scatter.25.cloned.1.call-start = ((), (), s32[]{:S(2)}) async-start(), calls=%async_computation.20 | async-start | bytes 10240000 | tf_op jit(solution)/shard_map/reduce_scatter | solution.py:604
  1763.5 237.1 %reduce-scatter.23.cloned.1.call-start = ((), (), s32[]{:S(2)}) async-start(), calls=%async_computation.19 | async-start | bytes 10240000 | tf_op jit(solution)/shard_map/reduce_scatter | solution.py:604
  1764.2 318.7 %reduce-scatter.21.cloned.1.call-start = ((), (), s32[]{:S(2)}) async-start(), calls=%async_computation.18 | async-start | bytes 10240000 | tf_op jit(solution)/shard_map/reduce_scatter | solution.py:604
  1765.0 400.2 %reduce-scatter.19.cloned.1.call-start = ((), (), s32[]{:S(2)}) async-start(), calls=%async_computation.17 | async-start | bytes 10240000 | tf_op jit(solution)/shard_map/reduce_scatter | solution.py:604
  1765.7 2.7 copy-start.2
  1765.7 2.7 copy-start.1
  1765.7 481.7 %reduce-scatter.17.cloned.1.call-start = ((), (), s32[]{:S(2)}) async-start(), calls=%async_computation.16 | async-start | bytes 10240000 | tf_op jit(solution)/shard_map/reduce_scatter | solution.py:604
  1766.3 563.4 %reduce-scatter.15.cloned.1.call-start = ((), (), s32[]{:S(2)}) async-start(), calls=%async_computation.15 | async-start | bytes 10240000 | tf_op jit(solution)/shard_map/reduce_scatter | solution.py:604
  1767.1 644.8 %reduce-scatter.13.cloned.1.call-start = ((), (), s32[]{:S(2)}) async-start(), calls=%async_computation.14 | async-start | bytes 10240000 | tf_op jit(solution)/shard_map/reduce_scatter | solution.py:604
  1767.6 726.5 %reduce-scatter.11.cloned.1.call-start = ((), (), s32[]{:S(2)}) async-start(), calls=%async_computation.13 | async-start | bytes 10240000 | tf_op jit(solution)/shard_map/reduce_scatter | solution.py:604
Sparse Core Ops, SparseCore 0:
  9.8 52.1 all-gather.8
  64.4 59.5 all-gather.6
  126.5 567.9 all-gather.4
  1661.9 62.7 reduce-scatter.28
  1763.0 72.9 reduce-scatter.26
  1839.0 79.1 reduce-scatter.24
  1921.4 79.1 reduce-scatter.22
  2003.7 79.1 reduce-scatter.20
  2086.0 79.1 reduce-scatter.18
  2168.2 79.1 reduce-scatter.16
  2250.5 79.1 reduce-scatter.14
  2332.7 79.1 reduce-scatter.12
  2415.0 79.1 reduce-scatter.10
